TPU v7x, 512 devices: a 8x2x16 block of a 8x8x16 slice. The times are simulated.
512 devices in a mesh: groups: 2 (over y), aa: 16 (over z), ba: 16 (over x, core).
Axes of the slice: x: 8, y: 2, z: 16, core: 2. Of those that a mesh axis runs over, the one named last changes fastest.
The devices are a block of a 8x8x16 slice.
Arguments:
- alignment_state: bfloat16 [256, 512, 256], P(('groups', 'aa'), 'ba'), parts along dimension 0, may hold values from -1.5 to 1.5
- pair_state: bfloat16 [1024, 512, 128], P(('groups', 'aa'), 'ba'), parts along dimension 0, may hold values from -1.796875 to 1.796875
- alignment_mask: int32 [256, 512], P(('groups', 'aa'), 'ba'), parts along dimension 0, may hold values from 0 to 1, as said below
- left_weight: bfloat16 [256, 32], replicated, may hold values from -0.375 to 0.375
- right_weight: bfloat16 [256, 32], replicated, may hold values from -0.375 to 0.375
- outer_output_weight: bfloat16 [1024, 128], replicated, may hold values from -0.75 to 0.75
- pair_bias_weight: bfloat16 [128, 8], replicated, may hold values from -40 to 40
- query_weight: bfloat16 [256, 256], replicated, may hold values from -0.375 to 0.375
- key_weight: bfloat16 [256, 256], replicated, may hold values from -0.375 to 0.375
- value_weight: bfloat16 [256, 256], replicated, may hold values from -0.375 to 0.375
- gate_weight: bfloat16 [256, 256], replicated, may hold values from -0.375 to 0.375
- output_weight: bfloat16 [256, 256], replicated, may hold values from -1.5 to 1.5
- up_weight: bfloat16 [256, 1024], replicated, may hold values from -0.375 to 0.375
- down_weight: bfloat16 [1024, 256], replicated, may hold values from -0.1875 to 0.1875
Outputs:
- alignment_output: bfloat16 [256, 512, 256], P(('groups', 'aa'), 'ba'), parts along dimension 0
- pair_output: bfloat16 [1024, 512, 128], P(('groups', 'aa'), 'ba'), parts along dimension 0
There are 2 independent parts, one for each index of `groups`. A program takes and returns all parts, laid end to end along the dimension named above; an argument that names none is the same for every part. Nothing has to cross between parts.
Inputs may be any that keep to these rules, and one draw needn't show every extreme that they name: `alignment_mask`: every residue of the first sequence is kept (mask 1); other entries are kept at random.
All inputs are finite; a program needn't handle non-finite values.
Results may differ from a plain program's by a relative error of at most 0.013.
The roundings to bfloat16 on the way count: a program that leaves them out, or rounds other values in their place, can miss the bound.
Values may be sent and summed in bfloat16 or wider, within the bound.
A program may use at most 128 MiB of HBM per device.

v0:
```python
import functools

import jax
import jax.numpy as jnp
from jax import lax
from jax.experimental import pallas as pl
from jax.experimental.pallas import tpu as pltpu
from jax.sharding import PartitionSpec as P

F32 = jnp.float32
BF16 = jnp.bfloat16
NT = (((1,), (1,)), ((), ()))


def mm(x, y):
    return jnp.dot(x, y, preferred_element_type=F32)


def mm_nt(x, y):
    return lax.dot_general(x, y, NT, preferred_element_type=F32)


def row_norm(values):
    center = values - jnp.mean(values, axis=-1, keepdims=True)
    spread = jnp.mean(center * center, axis=-1, keepdims=True)
    return center * lax.rsqrt(spread + 1e-05)


def near_to_far(t):
    return ((t + 1) // 2) * (2 * (t % 2) - 1)


def body(
    n,
    state_ref,
    pair_ref,
    mask_ref,
    left_ref,
    right_ref,
    outer_ref,
    pbw_ref,
    wq_ref,
    wk_ref,
    wv_ref,
    wg_ref,
    wo_ref,
    up_ref,
    down_ref,
    msa_out,
    pair_out,
    rows,
    nf,
    lx,
    lz,
    rz,
    tz,
    bx,
    lf,
    rf,
    rt,
    rt2,
    lb,
    wf,
    bd,
    lhs,
    upd,
    pn,
    bi,
    bh,
    kv,
    sc,
    qs,
    gs,
    vm,
    gated,
    lx_s,
    lx_r,
    lz_s,
    lz_r,
    rz_s,
    rz_r,
    x1_s,
    x1_r,
    xf_s,
    xf_r,
    tz_s,
    tz_r,
    bx_s,
    bx_r,
):
    a = lax.axis_index("aa")
    b = lax.axis_index("ba")
    core = b % 2
    chip = b // 2
    chips = n // 2
    partner = chip * 2 + 1 - core
    ns = state_ref.shape[0]
    res = state_ref.shape[1]
    ch = state_ref.shape[2]
    half = ns // 2
    opm = left_ref.shape[1]
    cz = pair_ref.shape[2]
    heads = pbw_ref.shape[1]
    wide = res * opm
    per = 128 // opm

    def row_peer(t):
        c = (chip + near_to_far(t // 2) + chips) % chips
        return c * 2 + t % 2

    def col_peer(t):
        return (a + near_to_far(t) + n) % n

    barrier = pltpu.get_barrier_semaphore()

    def greet(t, _):
        pl.semaphore_signal(
            barrier, inc=1, device_id={"ba": (b + t) % n}, device_id_type=pl.DeviceIdType.MESH
        )
        pl.semaphore_signal(
            barrier, inc=1, device_id={"aa": (a + t) % n}, device_id_type=pl.DeviceIdType.MESH
        )
        return 0

    lax.fori_loop(1, n, greet, 0)

    state = state_ref[...].reshape(ns * res, ch).astype(F32)
    normed = row_norm(state).astype(BF16)
    rows[:, b] = normed.reshape(ns, res, ch)
    for q in range(ch // 128):
        nf[q] = normed[:, q * 128 : (q + 1) * 128].astype(F32)
    by_res = jnp.concatenate(
        [
            jnp.concatenate(
                [nf[q, pl.ds(r, ns, stride=res), :] for r in range(res)], axis=0
            ).astype(BF16)
            for q in range(ch // 128)
        ],
        axis=1,
    )
    lane = lax.broadcasted_iota(jnp.int32, (opm, 128), 1)
    line = lax.broadcasted_iota(jnp.int32, (opm, 128), 0)
    rep = jnp.where(lane % opm == line, 1.0, 0.0).astype(BF16)
    seg = lax.broadcasted_iota(jnp.int32, (ns, 128), 1) // opm
    keep = mask_ref[...].astype(F32).astype(BF16)
    lane_w = lax.broadcasted_iota(jnp.int32, (res, wide), 1) // opm
    line_w = lax.broadcasted_iota(jnp.int32, (res, wide), 0)
    keep_wide = mm(keep, jnp.where(lane_w == line_w, 1.0, 0.0).astype(BF16))
    keep_rep = mm(keep, rep).astype(BF16)

    def pick(parts):
        out = parts[0]
        for k in range(1, per):
            out = jnp.where(seg == k, parts[k], out)
        return out

    def factor(w_ref):
        w4 = mm(w_ref[...], rep).astype(BF16)
        y = mm(by_res, w4)
        cols = [
            pick([y[(q * per + k) * ns : (q * per + k + 1) * ns] for k in range(per)])
            for q in range(res // per)
        ]
        return (jnp.concatenate(cols, axis=1) * keep_wide).astype(BF16)

    lx[b, :, :wide] = factor(left_ref)
    lx[b, :, wide:] = keep_rep
    rz[a, :, :wide] = factor(right_ref)
    rz[a, :, wide:] = keep_rep

    pl.semaphore_wait(barrier, 2 * (n - 1))

    def to_row(buf, src, i, who, ss, rs):
        return pltpu.make_async_remote_copy(
            src_ref=src,
            dst_ref=buf,
            send_sem=ss.at[who],
            recv_sem=rs.at[i],
            device_id={"ba": who},
            device_id_type=pl.DeviceIdType.MESH,
        )

    def to_col(buf, src, i, who, ss, rs):
        return pltpu.make_async_remote_copy(
            src_ref=src,
            dst_ref=buf,
            send_sem=ss.at[who],
            recv_sem=rs.at[i],
            device_id={"aa": who},
            device_id_type=pl.DeviceIdType.MESH,
        )

    def lx_copy(i, who):
        return to_row(lx.at[i], lx.at[i], i, who, lx_s, lx_r)

    def rz_copy(i, who):
        return to_col(rz.at[i], rz.at[i], i, who, rz_s, rz_r)

    def lz_copy(i, who):
        return to_col(lz.at[i], lx.at[who], i, who, lz_s, lz_r)

    def tz_copy(i, who):
        return to_col(tz.at[i], tz.at[i], i, who, tz_s, tz_r)

    def bx_copy(i, who):
        return to_row(bx.at[i], tz.at[who], i, who, bx_s, bx_r)

    def x1_copy(i, who, c):
        part = rows.at[pl.ds(half * c, half), i]
        return to_row(part, part, i, who, x1_s, x1_r)

    def xf_copy(i):
        part = rows.at[pl.ds(half * core, half), i]
        return pltpu.make_async_remote_copy(
            src_ref=part,
            dst_ref=part,
            send_sem=xf_s.at[i],
            recv_sem=xf_r.at[i],
            device_id={"ba": partner},
            device_id_type=pl.DeviceIdType.MESH,
        )

    def in_part(i):
        part = rows.at[pl.ds(half * (1 - core), half), i]
        return pltpu.make_async_remote_copy(
            src_ref=part,
            dst_ref=part,
            send_sem=xf_s.at[i],
            recv_sem=xf_r.at[i],
            device_id={"ba": partner},
            device_id_type=pl.DeviceIdType.MESH,
        )

    def start_lr(t, _):
        far = n - 1 - t
        lx_copy(b, row_peer(far)).start()
        rz_copy(a, col_peer(far)).start()
        return 0

    def start_l_off(t, _):
        lx_copy(b, row_peer(n - 1 - t)).start()
        return 0

    def start_r(t, _):
        rz_copy(a, col_peer(n - 1 - t)).start()
        return 0

    lx_copy(b, partner).start()
    lax.fori_loop(0, n - 2, start_l_off, 0)
    lax.fori_loop(0, n - 1, start_r, 0)

    def start_x(t, _):
        who = row_peer(n - 1 - t)
        x1_copy(b, who, who % 2).start()
        return 0

    lax.fori_loop(0, n - 2, start_x, 0)
    x1_copy(b, partner, 1 - core).start()
    xf_copy(b).start()

    wf[...] = outer_ref[...].astype(F32)

    def build(d, _):
        w = wf[pl.ds(d, opm, stride=opm), :].astype(BF16)
        zero = jnp.zeros_like(w)
        for k in range(per):
            bd[pl.ds(d * 128 + k * opm, opm), :] = jnp.concatenate(
                [w if m == k else zero for m in range(per)], axis=1
            )
        return 0

    lax.fori_loop(0, opm, build, 0)

    def pass_left(t, _):
        i = row_peer(t)

        @pl.when(i != b)
        def _():
            lx_copy(i, b).wait_recv()

        @pl.when(i != a)
        def _():
            lz_copy(a, i).start()

        @pl.when(i == a)
        def _():
            lz[a] = lx[i]

        return 0

    lax.fori_loop(0, n, pass_left, 0)

    qs[...] = (mm(normed, wq_ref[...]) * ((ch // heads) ** (-0.5))).astype(BF16)
    gs[...] = jax.nn.sigmoid(mm(normed, wg_ref[...]))
    for q in range(n // per):
        vm[:, q * 128 : (q + 1) * 128] = pick(
            [lx[q * per + k, :, wide:].astype(F32) for k in range(per)]
        )

    def land_right(t, _):
        i = col_peer(t)

        @pl.when(i != a)
        def _():
            rz_copy(i, a).wait_recv()

        rf[pl.ds(pl.multiple_of(i * ns, ns), ns), :] = rz[i].astype(F32)
        return 0

    lax.fori_loop(0, n, land_right, 0)
    for q in range(wide // 128):
        rt[q * 128 : (q + 1) * 128, :] = rf[:, q * 128 : (q + 1) * 128].T

    def reorder(d, _):
        rt2[pl.ds(pl.multiple_of(d * res, res), res), :] = rt[
            pl.ds(d, res, stride=opm), :
        ].astype(BF16)
        return 0

    lax.fori_loop(0, opm, reorder, 0)

    def land_left(t, _):
        i = col_peer(t)

        @pl.when(i != a)
        def _():
            lz_copy(i, a).wait_recv()

        lf[pl.ds(pl.multiple_of(i * ns, ns), ns), :] = lz[i].astype(F32)
        return 0

    lax.fori_loop(0, n, land_left, 0)

    groups = res // per
    for g in range(groups):
        lb[g] = lf[:, g * 128 : (g + 1) * 128].astype(BF16)

    def outer(g, _):
        block = mm(rt2[...], lb[g]).astype(BF16)
        for d in range(opm):
            lhs[pl.ds(pl.multiple_of(g * res, res), res), d * 128 : (d + 1) * 128] = block[
                d * res : (d + 1) * res
            ]
        return 0

    lax.fori_loop(0, groups, outer, 0)
    upd[...] = mm(lhs[...], bd[...])
    count = mm(rf[:, wide:].T.astype(BF16), lf[:, wide:].astype(BF16))
    inverse = 1.0 / count[:res]
    for i in range(res):
        block = upd[(i // per) * res : (i // per + 1) * res, (i % per) * 128 : (i % per + 1) * 128]
        fresh = (pair_ref[i].astype(F32) + block * inverse[:, i : i + 1]).astype(BF16)
        pair_out[i] = fresh
        pn[i * res : (i + 1) * res, :] = row_norm(fresh.astype(F32)).astype(BF16)
    eye_l = lax.broadcasted_iota(jnp.int32, (heads, heads), 1)
    eye_s = lax.broadcasted_iota(jnp.int32, (heads, heads), 0)
    eye = jnp.where(eye_l == eye_s, 1.0, 0.0).astype(BF16)
    pbw_t = mm_nt(eye, pbw_ref[...]).astype(BF16)
    tz[a] = mm_nt(pbw_t, pn[...])

    def start_bias(t, _):
        tz_copy(a, col_peer(n - 1 - t)).start()
        return 0

    lax.fori_loop(0, n - 1, start_bias, 0)

    def pass_rows(t, _):
        i = row_peer(t)
        x1_copy(i, b, core).wait_recv()
        xf_copy(i).start()
        return 0

    x1_copy(partner, b, core).wait_recv()
    lax.fori_loop(2, n, pass_rows, 0)
    in_part(partner).wait_recv()

    def land_rows(t, _):
        in_part(row_peer(t)).wait_recv()
        return 0

    lax.fori_loop(2, n, land_rows, 0)

    head_lane = lax.broadcasted_iota(jnp.int32, (res, ch), 1) // (ch // heads)

    def score(s, _):
        x = rows[s].reshape(n * res, ch)
        key = mm(x, wk_ref[...]).astype(BF16)
        kv[s] = mm(x, wv_ref[...]).astype(BF16)
        q = qs[pl.ds(pl.multiple_of(s * res, res), res), :].astype(F32)
        query = jnp.concatenate(
            [jnp.where(head_lane == h, q, 0.0) for h in range(heads)], axis=0
        ).astype(BF16)
        sc[s] = mm_nt(query, key)
        return 0

    lax.fori_loop(0, ns, score, 0)

    def pass_bias(t, _):
        i = col_peer(t)

        @pl.when(i != a)
        def _():
            tz_copy(i, a).wait_recv()

        @pl.when(i != b)
        def _():
            bx_copy(b, i).start()

        @pl.when(i == b)
        def _():
            bx[b] = tz[i]

        return 0

    lax.fori_loop(0, n, pass_bias, 0)

    def land_bias(t, _):
        i = (b + t) % n
        bx_copy(i, b).wait_recv()
        return 0

    lax.fori_loop(1, n, land_bias, 0)

    for v in range(res // per):
        for q in range(n // per):
            cut = [bx[q * per + k, :, v * 128 : (v + 1) * 128] for k in range(per)]
            turned = [cut[0]] + [pltpu.roll(cut[k], opm * k, 1) for k in range(1, per)]
            for m in range(per):
                mixed = pick([turned[(k - m) % per] for k in range(per)])
                if m:
                    mixed = pltpu.roll(mixed, 128 - opm * m, 1)
                i = v * per + m
                bi[q, i * heads : (i + 1) * heads, :] = mixed
    for h in range(heads):
        for q in range(n // per):
            bh[h * res : (h + 1) * res, q * 128 : (q + 1) * 128] = bi[
                q, pl.ds(h, res, stride=heads), :
            ]

    def attend(s, _):
        valid = vm[pl.ds(s, 1), :]
        scores = jnp.where(valid > 0, sc[s] + bh[...], -1000000000.0)
        top = jnp.max(scores, axis=-1, keepdims=True)
        raw = jnp.exp(scores - top)
        mass = jnp.sum(raw, axis=-1, keepdims=True)
        mixed = mm(raw.astype(BF16), kv[s]) / mass
        out = mixed[:res]
        for h in range(1, heads):
            out = jnp.where(head_lane == h, mixed[h * res : (h + 1) * res], out)
        at = pl.ds(pl.multiple_of(s * res, res), res)
        gated[at, :] = (out * gs[at, :]).astype(BF16)
        return 0

    lax.fori_loop(0, ns, attend, 0)

    middle = state + mm(gated[...], wo_ref[...])
    hidden = jnp.maximum(mm(row_norm(middle).astype(BF16), up_ref[...]), 0.0).astype(BF16)
    final = middle + mm(hidden, down_ref[...])
    msa_out[...] = final.astype(BF16).reshape(ns, res, ch)

    def drain(t, _):
        who = (b + t) % n
        lx_copy(b, who).wait_send()
        bx_copy(b, who).wait_send()
        up_to = (a + t) % n
        rz_copy(a, up_to).wait_send()
        lz_copy(a, up_to).wait_send()
        tz_copy(a, up_to).wait_send()
        x1_copy(b, who, who % 2).wait_send()
        return 0

    lax.fori_loop(1, n, drain, 0)

    def drain_rows(t, _):
        xf_copy(row_peer(t)).wait_send()
        return 0

    lax.fori_loop(2, n, drain_rows, 0)
    xf_copy(b).wait_send()


def per_device(n, *args):
    state, pair, mask, left, _, _, pbw = args[:7]
    ns, res, ch = state.shape
    opm, heads, cz = left.shape[1], pbw.shape[1], pair.shape[2]
    wide = res * opm
    per = 128 // opm
    groups = res // per
    keys = n * res
    dma = pltpu.SemaphoreType.DMA((n,))
    vmem = pl.BlockSpec(memory_space=pltpu.VMEM)
    return tuple(
        pl.pallas_call(
            functools.partial(body, n),
            out_shape=(
                jax.ShapeDtypeStruct(state.shape, BF16),
                jax.ShapeDtypeStruct(pair.shape, BF16),
            ),
            in_specs=[vmem] * len(args),
            out_specs=(vmem, vmem),
            scratch_shapes=[
                pltpu.VMEM((ns, n, res, ch), BF16),
                pltpu.VMEM((ch // 128, ns * res, 128), F32),
                pltpu.VMEM((n, ns, wide + 128), BF16),
                pltpu.VMEM((n, ns, wide + 128), BF16),
                pltpu.VMEM((n, ns, wide + 128), BF16),
                pltpu.VMEM((n, heads, res * res), F32),
                pltpu.VMEM((n, heads, res * res), F32),
                pltpu.VMEM((n * ns, wide + 128), F32),
                pltpu.VMEM((n * ns, wide + 128), F32),
                pltpu.VMEM((wide, n * ns), F32),
                pltpu.VMEM((wide, n * ns), BF16),
                pltpu.VMEM((groups, n * ns, 128), BF16),
                pltpu.VMEM((opm * opm, cz), F32),
                pltpu.VMEM((opm * 128, per * cz), BF16),
                pltpu.VMEM((groups * res, opm * 128), BF16),
                pltpu.VMEM((groups * res, per * cz), F32),
                pltpu.VMEM((res * res, cz), BF16),
                pltpu.VMEM((keys // 128, res * heads, 128), F32),
                pltpu.VMEM((heads * res, keys), F32),
                pltpu.VMEM((ns, keys, ch), BF16),
                pltpu.VMEM((ns, heads * res, keys), F32),
                pltpu.VMEM((ns * res, ch), BF16),
                pltpu.VMEM((ns * res, ch), F32),
                pltpu.VMEM((ns, keys), F32),
                pltpu.VMEM((ns * res, ch), BF16),
            ]
            + [dma] * 14,
            compiler_params=pltpu.CompilerParams(collective_id=0, has_side_effects=True),
        )(*args)
    )


def solution(mesh):
    spec = P(("groups", "aa"), "ba", None)
    return jax.shard_map(
        functools.partial(per_device, mesh.shape["ba"]),
        mesh=mesh,
        in_specs=(spec, spec, P(("groups", "aa"), "ba")) + (P(),) * 11,
        out_specs=(spec, spec),
        check_vma=False,
    )
```

profile of v0, /device:TPU:87, one launch (start us, length us, event | category | flops | bytes accessed | tf_op | source)
XLA Modules:
  0.0 129.5 jit_solution(3759744571758778977)
XLA Ops:
  0.6 0.0 copy-start.1
  0.6 1.4 %copy.18.pbw_ref = bf16[128,8]{1,0:T(8,128)(2,1)} copy(bf16[128,8]{0,1:T(8,128)(2,1)} %param.20) | data formatting | bytes 4096 | tf_op args[6]
  2.0 0.0 copy-done.1
  2.0 0.0 copy-start.2
  2.0 0.7 copy.16.left_ref
  2.8 0.0 copy-done.2
  2.8 0.7 copy.17.right_ref
  3.5 123.6 %shard_map.149 = (bf16[8,32,256]{2,1,0:T(8,128)(2,1)}, bf16[32,32,128]{2,1,0:T(8,128)(2,1)}) custom-call(bf16[8,32,256]{2,1,0:T(8,128)(2,1)} %state_ref.1, bf16[32,32,128]{2,1,0:T(8,128)(2,1)} %pair_ref.1, s32[8,32]{1,0:T(8,128)} %mask_ref.1, bf16[256,32]{1,0:T(8,128)(2,1)} %copy.16.left_ref, bf16[256,32]{1,0:T(8,128)(2,1)} %copy.17.right_ref, ...), custom_call_target="tpu_custom_call" | custom-call | tf_op jit(solution)/shard_map/pallas_call | solution.py:493
  127.2 0.0 copy-start
  127.2 1.6 %copy.21 = bf16[8,32,256]{2,1,0:T(8,128)(2,1)} copy(bf16[8,32,256]{2,1,0:T(8,128)(2,1)} %get-tuple-element.4) | data formatting | bytes 262144
  128.8 0.0 copy-done
  128.8 0.7 copy.22
Async XLA Ops:
  0.6 1.4 %copy-start.1 = (bf16[256,32]{0,1:T(8,128)(2,1)S(1)}, bf16[256,32]{0,1:T(8,128)(2,1)}, u32[]{:S(2)}) copy-start(bf16[256,32]{0,1:T(8,128)(2,1)} %param.17) | copy-start | bytes 49156
  2.0 0.7 copy-start.2
  127.2 1.6 %copy-start = (bf16[32,32,128]{2,1,0:T(8,128)(2,1)S(1)}, bf16[32,32,128]{2,1,0:T(8,128)(2,1)}, u32[]{:S(2)}) copy-start(bf16[32,32,128]{2,1,0:T(8,128)(2,1)} %get-tuple-element.5) | copy-start | bytes 786436
where the time goes:
time: 130 us; the launch traced here: 129 us
  Pallas kernels  124 us (95%)
  local copies, waits for them, and re-layouts  5.18 us (4%)
    pallas_call x1, Pallas kernels, per_device(): pl.pallas_call(functools.partial(body, n), out_shape=(jax.ShapeDtypeStruc...  124 us
    unnamed x11, local copies, waits for them, and re-layouts  5.18 us

commit v1 on v0

--- a/solution.py
+++ b/solution.py
@@ -33,12 +33,23 @@
 def body(
     n,
     state_ref,
-    pair_ref,
+    pair_hbm,
     mask_ref,
     left_ref,
     right_ref,
+    outer_hbm,
+    pbw_ref,
+    wq_hbm,
+    wk_hbm,
+    wv_hbm,
+    wg_hbm,
+    wo_hbm,
+    up_hbm,
+    down_hbm,
+    msa_hbm_out,
+    pair_hbm_out,
+    pair_ref,
     outer_ref,
-    pbw_ref,
     wq_ref,
     wk_ref,
     wv_ref,
@@ -46,10 +57,13 @@
     wo_ref,
     up_ref,
     down_ref,
+    pair_out,
     msa_out,
-    pair_out,
+    load_sem,
+    store_sem,
     rows,
     nf,
+    ls,
     lx,
     lz,
     rz,
@@ -77,10 +91,13 @@
     lx_r,
     lz_s,
     lz_r,
+    lf_s,
+    lf_r,
     rz_s,
     rz_r,
     x1_s,
     x1_r,
+    xr_s,
     xf_s,
     xf_r,
     tz_s,
@@ -98,11 +115,19 @@
     res = state_ref.shape[1]
     ch = state_ref.shape[2]
     half = ns // 2
-    opm = left_ref.shape[1]
+    opm = left_ref.shape[0]
     cz = pair_ref.shape[2]
-    heads = pbw_ref.shape[1]
+    heads = pbw_ref.shape[0]
     wide = res * opm
     per = 128 // opm
+    span = wide // 2
+
+    hbm = (outer_hbm, wq_hbm, wg_hbm, pair_hbm, wk_hbm, wv_hbm, wo_hbm, up_hbm, down_hbm)
+    local = (outer_ref, wq_ref, wg_ref, pair_ref, wk_ref, wv_ref, wo_ref, up_ref, down_ref)
+    loads = [
+        pltpu.make_async_copy(src, dst, load_sem.at[k])
+        for k, (src, dst) in enumerate(zip(hbm, local))
+    ]
 
     def row_peer(t):
         c = (chip + near_to_far(t // 2) + chips) % chips
@@ -123,6 +148,9 @@
         return 0
 
     lax.fori_loop(1, n, greet, 0)
+
+    for load in loads:
+        load.start()
 
     state = state_ref[...].reshape(ns * res, ch).astype(F32)
     normed = row_norm(state).astype(BF16)
@@ -141,6 +169,9 @@
     lane = lax.broadcasted_iota(jnp.int32, (opm, 128), 1)
     line = lax.broadcasted_iota(jnp.int32, (opm, 128), 0)
     rep = jnp.where(lane % opm == line, 1.0, 0.0).astype(BF16)
+    lane_t = lax.broadcasted_iota(jnp.int32, (128, opm), 1)
+    line_t = lax.broadcasted_iota(jnp.int32, (128, opm), 0)
+    rep_t = jnp.where(line_t % opm == lane_t, 1.0, 0.0).astype(BF16)
     seg = lax.broadcasted_iota(jnp.int32, (ns, 128), 1) // opm
     keep = mask_ref[...].astype(F32).astype(BF16)
     lane_w = lax.broadcasted_iota(jnp.int32, (res, wide), 1) // opm
@@ -155,16 +186,18 @@
         return out
 
     def factor(w_ref):
-        w4 = mm(w_ref[...], rep).astype(BF16)
-        y = mm(by_res, w4)
+        y = mm_nt(by_res, mm(rep_t, w_ref[...]).astype(BF16))
         cols = [
             pick([y[(q * per + k) * ns : (q * per + k + 1) * ns] for k in range(per)])
             for q in range(res // per)
         ]
         return (jnp.concatenate(cols, axis=1) * keep_wide).astype(BF16)
 
-    lx[b, :, :wide] = factor(left_ref)
-    lx[b, :, wide:] = keep_rep
+    left = factor(left_ref)
+    for k in range(2):
+        ls[k, :, :span] = left[:, k * span : (k + 1) * span]
+        ls[k, :, span:] = keep_rep
+    lx[b] = ls[core]
     rz[a, :, :wide] = factor(right_ref)
     rz[a, :, wide:] = keep_rep
 
@@ -191,19 +224,121 @@
         )
 
     def lx_copy(i, who):
-        return to_row(lx.at[i], lx.at[i], i, who, lx_s, lx_r)
-
-    def rz_copy(i, who):
-        return to_col(rz.at[i], rz.at[i], i, who, rz_s, rz_r)
+        return to_row(lx.at[i], ls.at[who % 2], i, who, lx_s, lx_r)
 
     def lz_copy(i, who):
-        return to_col(lz.at[i], lx.at[who], i, who, lz_s, lz_r)
-
-    def tz_copy(i, who):
-        return to_col(tz.at[i], tz.at[i], i, who, tz_s, tz_r)
+        return to_col(lz.at[i, core], lx.at[who], i, who, lz_s, lz_r)
+
+    def lf_copy(i, k, src=None):
+        part = lz.at[i, k]
+        return pltpu.make_async_remote_copy(
+            src_ref=part if src is None else src,
+            dst_ref=part,
+            send_sem=lf_s.at[i],
+            recv_sem=lf_r.at[i],
+            device_id={"ba": partner},
+            device_id_type=pl.DeviceIdType.MESH,
+        )
 
     def bx_copy(i, who):
         return to_row(bx.at[i], tz.at[who], i, who, bx_s, bx_r)
+
+    turn = n // 2
+
+    def hop(buf, ss, rs, d, step, way):
+        i = (a + n - way * d) % n
+        part = buf.at[i]
+        return pltpu.make_async_remote_copy(
+            src_ref=part,
+            dst_ref=part,
+            send_sem=ss.at[d + step - 1 if way > 0 else turn + d + step - 1],
+            recv_sem=rs.at[i],
+            device_id={"aa": (a + n + way * step) % n},
+            device_id_type=pl.DeviceIdType.MESH,
+        )
+
+    def spread(buf, ss, rs, d, reach, wait=False):
+        def one(step, way):
+            copy = hop(buf, ss, rs, d, step, way)
+            if wait:
+                copy.wait_send()
+            else:
+                copy.start()
+
+        for step in range(min(reach, turn - d), 0, -1):
+            for way in (1, -1):
+                if d + step < turn:
+                    one(step, way)
+                else:
+                    pl.when(core == (1 - way) // 2)(functools.partial(one, step, way))
+
+    def ring(buf, ss, rs, reach, first, last, landed):
+        for d in range(first, last + 1):
+            for way in (1, -1):
+                if d < turn or way > 0:
+                    hop(buf, ss, rs, d, 0, way).wait_recv()
+            if d % reach == 0:
+                spread(buf, ss, rs, d, reach)
+            for way in (1, -1):
+                if d < turn or way > 0:
+                    landed((a + n - way * d) % n)
+
+    def ring_sent(buf, ss, rs, reach):
+        for d in range(0, turn, reach):
+            spread(buf, ss, rs, d, reach, wait=True)
+
+    across = chips // 2
+
+    def x_to(i, c, step, way, sem):
+        part = rows.at[pl.ds(half * c, half), i]
+        who = ((chip + chips + way * step) % chips) * 2 + c
+        return pltpu.make_async_remote_copy(
+            src_ref=part,
+            dst_ref=part,
+            send_sem=sem,
+            recv_sem=x1_r.at[i],
+            device_id={"ba": who},
+            device_id_type=pl.DeviceIdType.MESH,
+        )
+
+    def x_first(wait=False):
+        def one(step, way, c):
+            k = (2 * step - 2 + (1 - way) // 2) * 2 + c
+            copy = x_to(b, c, step, way, x1_s.at[k])
+            if wait:
+                copy.wait_send()
+            else:
+                copy.start()
+
+        for step in range(min(2, across), 0, -1):
+            for way in (1, -1):
+                for c in range(2):
+                    if step < across:
+                        one(step, way, c)
+                    else:
+                        pl.when(core == (1 - way) // 2)(functools.partial(one, step, way, c))
+
+    def x_on(wait=False):
+        for step in range(min(2, across - 2), 0, -1):
+            for way in (1, -1):
+                for c in range(2):
+                    if 2 + step < across or c == (1 - way) // 2:
+                        i = ((chip + chips - 2 * way) % chips) * 2 + c
+                        k = (2 * step - 2 + (1 - way) // 2) * 2 + c
+                        copy = x_to(i, core, step, way, xr_s.at[k])
+                        if wait:
+                            copy.wait_send()
+                        else:
+                            copy.start()
+
+    def x_blocks(first, last):
+        return [
+            ((chip + chips - way * d) % chips) * 2 + c
+            for d in range(first, min(last, across) + 1)
+            for way in (1, -1)
+            if d < across or way > 0
+            for c in range(2)
+        ]
 
     def x1_copy(i, who, c):
         part = rows.at[pl.ds(half * c, half), i]
@@ -231,33 +366,15 @@
             device_id_type=pl.DeviceIdType.MESH,
         )
 
-    def start_lr(t, _):
-        far = n - 1 - t
-        lx_copy(b, row_peer(far)).start()
-        rz_copy(a, col_peer(far)).start()
-        return 0
-
     def start_l_off(t, _):
         lx_copy(b, row_peer(n - 1 - t)).start()
         return 0
 
-    def start_r(t, _):
-        rz_copy(a, col_peer(n - 1 - t)).start()
-        return 0
-
     lx_copy(b, partner).start()
     lax.fori_loop(0, n - 2, start_l_off, 0)
-    lax.fori_loop(0, n - 1, start_r, 0)
-
-    def start_x(t, _):
-        who = row_peer(n - 1 - t)
-        x1_copy(b, who, who % 2).start()
-        return 0
-
-    lax.fori_loop(0, n - 2, start_x, 0)
-    x1_copy(b, partner, 1 - core).start()
-    xf_copy(b).start()
-
+    spread(rz, rz_s, rz_r, 0, 4)
+
+    loads[0].wait()
     wf[...] = outer_ref[...].astype(F32)
 
     def build(d, _):
@@ -284,30 +401,32 @@
 
         @pl.when(i == a)
         def _():
-            lz[a] = lx[i]
-
-        return 0
-
-    lax.fori_loop(0, n, pass_left, 0)
-
+            lz[a, core] = lx[i]
+            lf_copy(a, core, lx.at[i]).start()
+
+        return 0
+
+    def land_right(i):
+        rf[pl.ds(pl.multiple_of(i * ns, ns), ns), :] = rz[i].astype(F32)
+
+    lax.fori_loop(0, n * 5 // 8, pass_left, 0)
+    land_right(a)
+    ring(rz, rz_s, rz_r, 4, 1, min(4, turn), land_right)
+    x_first()
+    x1_copy(b, partner, 1 - core).start()
+    xf_copy(b).start()
+    lax.fori_loop(n * 5 // 8, n, pass_left, 0)
+
+    loads[1].wait()
+    loads[2].wait()
     qs[...] = (mm(normed, wq_ref[...]) * ((ch // heads) ** (-0.5))).astype(BF16)
     gs[...] = jax.nn.sigmoid(mm(normed, wg_ref[...]))
     for q in range(n // per):
         vm[:, q * 128 : (q + 1) * 128] = pick(
-            [lx[q * per + k, :, wide:].astype(F32) for k in range(per)]
-        )
-
-    def land_right(t, _):
-        i = col_peer(t)
-
-        @pl.when(i != a)
-        def _():
-            rz_copy(i, a).wait_recv()
-
-        rf[pl.ds(pl.multiple_of(i * ns, ns), ns), :] = rz[i].astype(F32)
-        return 0
-
-    lax.fori_loop(0, n, land_right, 0)
+            [lx[q * per + k, :, span:].astype(F32) for k in range(per)]
+        )
+
+    ring(rz, rz_s, rz_r, 4, 5, turn, land_right)
     for q in range(wide // 128):
         rt[q * 128 : (q + 1) * 128, :] = rf[:, q * 128 : (q + 1) * 128].T
 
@@ -319,21 +438,33 @@
 
     lax.fori_loop(0, opm, reorder, 0)
 
+    def half_left(i, k):
+        block = lz[i, k].astype(F32)
+        at = pl.ds(pl.multiple_of(i * ns, ns), ns)
+        lf[k, at, :] = block
+
+    def share_left(t, _):
+        i = col_peer(t)
+        lz_copy(i, a).wait_recv()
+        lf_copy(i, core).start()
+        half_left(i, core)
+        return 0
+
+    half_left(a, core)
+    lax.fori_loop(1, n, share_left, 0)
+
     def land_left(t, _):
         i = col_peer(t)
-
-        @pl.when(i != a)
-        def _():
-            lz_copy(i, a).wait_recv()
-
-        lf[pl.ds(pl.multiple_of(i * ns, ns), ns), :] = lz[i].astype(F32)
+        lf_copy(i, 1 - core).wait_recv()
+        half_left(i, 1 - core)
         return 0
 
     lax.fori_loop(0, n, land_left, 0)
 
     groups = res // per
     for g in range(groups):
-        lb[g] = lf[:, g * 128 : (g + 1) * 128].astype(BF16)
+        at = (g % (groups // 2)) * 128
+        lb[g] = lf[g // (groups // 2), :, at : at + 128].astype(BF16)
 
     def outer(g, _):
         block = mm(rt2[...], lb[g]).astype(BF16)
@@ -345,33 +476,54 @@
 
     lax.fori_loop(0, groups, outer, 0)
     upd[...] = mm(lhs[...], bd[...])
-    count = mm(rf[:, wide:].T.astype(BF16), lf[:, wide:].astype(BF16))
+
+    def pass_rows(first, last):
+        for i in x_blocks(first, last):
+            x1_copy(i, b, core).wait_recv()
+            if (first, last) == (1, 2):
+                continue
+            xf_copy(i).start()
+
+    pass_rows(1, 2)
+    x_on()
+    for i in x_blocks(1, 2):
+        xf_copy(i).start()
+    count = mm(rf[:, wide:].T.astype(BF16), lf[0, :, span:].astype(BF16))
     inverse = 1.0 / count[:res]
-    for i in range(res):
-        block = upd[(i // per) * res : (i // per + 1) * res, (i % per) * 128 : (i % per + 1) * 128]
-        fresh = (pair_ref[i].astype(F32) + block * inverse[:, i : i + 1]).astype(BF16)
-        pair_out[i] = fresh
-        pn[i * res : (i + 1) * res, :] = row_norm(fresh.astype(F32)).astype(BF16)
-    eye_l = lax.broadcasted_iota(jnp.int32, (heads, heads), 1)
-    eye_s = lax.broadcasted_iota(jnp.int32, (heads, heads), 0)
-    eye = jnp.where(eye_l == eye_s, 1.0, 0.0).astype(BF16)
-    pbw_t = mm_nt(eye, pbw_ref[...]).astype(BF16)
-    tz[a] = mm_nt(pbw_t, pn[...])
-
-    def start_bias(t, _):
-        tz_copy(a, col_peer(n - 1 - t)).start()
-        return 0
-
-    lax.fori_loop(0, n - 1, start_bias, 0)
-
-    def pass_rows(t, _):
-        i = row_peer(t)
-        x1_copy(i, b, core).wait_recv()
-        xf_copy(i).start()
-        return 0
-
+    loads[3].wait()
+    step = 8
+    for at in range(0, res, step):
+        block = jnp.concatenate(
+            [
+                upd[i // per * res : (i // per + 1) * res, i % per * 128 : (i % per + 1) * 128]
+                * inverse[:, i : i + 1]
+                for i in range(at, at + step)
+            ],
+            axis=0,
+        )
+        old = pair_ref[at : at + step].reshape(step * res, cz).astype(F32)
+        fresh = (old + block).astype(BF16)
+        pair_out[at : at + step] = fresh.reshape(step, res, cz)
+        pn[at * res : (at + step) * res, :] = row_norm(fresh.astype(F32)).astype(BF16)
+    tz[a] = mm_nt(pbw_ref[...], pn[...])
+
+    spread(tz, tz_s, tz_r, 0, 3)
+    store = pltpu.make_async_copy(pair_out, pair_hbm_out, store_sem.at[0])
+    store.start()
+
+    def pass_bias(i):
+        @pl.when(i != b)
+        def _():
+            bx_copy(b, i).start()
+
+        @pl.when(i == b)
+        def _():
+            bx[b] = tz[i]
+
+    pass_bias(a)
+    ring(tz, tz_s, tz_r, 3, 1, min(3, turn), pass_bias)
+    pass_rows(3, across)
     x1_copy(partner, b, core).wait_recv()
-    lax.fori_loop(2, n, pass_rows, 0)
     in_part(partner).wait_recv()
 
     def land_rows(t, _):
@@ -379,8 +531,10 @@
         return 0
 
     lax.fori_loop(2, n, land_rows, 0)
-
     head_lane = lax.broadcasted_iota(jnp.int32, (res, ch), 1) // (ch // heads)
+
+    loads[4].wait()
+    loads[5].wait()
 
     def score(s, _):
         x = rows[s].reshape(n * res, ch)
@@ -393,36 +547,47 @@
         sc[s] = mm_nt(query, key)
         return 0
 
-    lax.fori_loop(0, ns, score, 0)
-
-    def pass_bias(t, _):
-        i = col_peer(t)
-
-        @pl.when(i != a)
-        def _():
-            tz_copy(i, a).wait_recv()
-
-        @pl.when(i != b)
-        def _():
-            bx_copy(b, i).start()
-
-        @pl.when(i == b)
-        def _():
-            bx[b] = tz[i]
-
-        return 0
-
-    lax.fori_loop(0, n, pass_bias, 0)
-
-    def land_bias(t, _):
-        i = (b + t) % n
-        bx_copy(i, b).wait_recv()
-        return 0
-
-    lax.fori_loop(1, n, land_bias, 0)
-
-    for v in range(res // per):
-        for q in range(n // per):
+    lax.fori_loop(0, half, score, 0)
+    ring(tz, tz_s, tz_r, 3, 4, min(6, turn), pass_bias)
+    lax.fori_loop(half, ns, score, 0)
+
+    def drain(t, _):
+        lx_copy(b, (b + t) % n).wait_send()
+        lz_copy(a, (a + t) % n).wait_send()
+        return 0
+
+    lax.fori_loop(1, n, drain, 0)
+
+    def drain_left(t, _):
+        lf_copy(t, core).wait_send()
+        return 0
+
+    lax.fori_loop(0, n, drain_left, 0)
+    ring_sent(rz, rz_s, rz_r, 4)
+    x_first(wait=True)
+    x_on(wait=True)
+    x1_copy(b, partner, 1 - core).wait_send()
+
+    def drain_rows(t, _):
+        xf_copy(row_peer(t)).wait_send()
+        return 0
+
+    lax.fori_loop(2, n, drain_rows, 0)
+    xf_copy(b).wait_send()
+    store.wait()
+    for load in loads[6:]:
+        load.wait()
+    ring(tz, tz_s, tz_r, 3, 7, turn, pass_bias)
+
+    for q in range(n // per):
+        for k in range(per):
+            i = q * per + k
+
+            @pl.when(i != b)
+            def _():
+                bx_copy(i, b).wait_recv()
+
+        for v in range(res // per):
             cut = [bx[q * per + k, :, v * 128 : (v + 1) * 128] for k in range(per)]
             turned = [cut[0]] + [pltpu.roll(cut[k], opm * k, 1) for k in range(1, per)]
             for m in range(per):
@@ -431,8 +596,7 @@
                     mixed = pltpu.roll(mixed, 128 - opm * m, 1)
                 i = v * per + m
                 bi[q, i * heads : (i + 1) * heads, :] = mixed
-    for h in range(heads):
-        for q in range(n // per):
+        for h in range(heads):
             bh[h * res : (h + 1) * res, q * 128 : (q + 1) * 128] = bi[
                 q, pl.ds(h, res, stride=heads), :
             ]
@@ -453,42 +617,37 @@
 
     lax.fori_loop(0, ns, attend, 0)
 
-    middle = state + mm(gated[...], wo_ref[...])
+    middle = state_ref[...].reshape(ns * res, ch).astype(F32) + mm(gated[...], wo_ref[...])
     hidden = jnp.maximum(mm(row_norm(middle).astype(BF16), up_ref[...]), 0.0).astype(BF16)
     final = middle + mm(hidden, down_ref[...])
     msa_out[...] = final.astype(BF16).reshape(ns, res, ch)
-
-    def drain(t, _):
-        who = (b + t) % n
-        lx_copy(b, who).wait_send()
-        bx_copy(b, who).wait_send()
-        up_to = (a + t) % n
-        rz_copy(a, up_to).wait_send()
-        lz_copy(a, up_to).wait_send()
-        tz_copy(a, up_to).wait_send()
-        x1_copy(b, who, who % 2).wait_send()
-        return 0
-
-    lax.fori_loop(1, n, drain, 0)
-
-    def drain_rows(t, _):
-        xf_copy(row_peer(t)).wait_send()
-        return 0
-
-    lax.fori_loop(2, n, drain_rows, 0)
-    xf_copy(b).wait_send()
+    store = pltpu.make_async_copy(msa_out, msa_hbm_out, store_sem.at[1])
+    store.start()
+    ring_sent(tz, tz_s, tz_r, 3)
+
+    def drain_bias(t, _):
+        bx_copy(b, (b + t) % n).wait_send()
+        return 0
+
+    lax.fori_loop(1, n, drain_bias, 0)
+    store.wait()
 
 
 def per_device(n, *args):
     state, pair, mask, left, _, _, pbw = args[:7]
     ns, res, ch = state.shape
     opm, heads, cz = left.shape[1], pbw.shape[1], pair.shape[2]
+    args = args[:3] + (left.T, args[4].T, args[5], pbw.T) + args[7:]
     wide = res * opm
+    span = wide // 2
     per = 128 // opm
     groups = res // per
     keys = n * res
     dma = pltpu.SemaphoreType.DMA((n,))
     vmem = pl.BlockSpec(memory_space=pltpu.VMEM)
+    far = pl.BlockSpec(memory_space=pl.ANY)
+    near = (0, 2, 3, 4, 6)
+    order = (1, 5, 7, 8, 9, 10, 11, 12, 13)
     return tuple(
         pl.pallas_call(
             functools.partial(body, n),
@@ -496,17 +655,23 @@
                 jax.ShapeDtypeStruct(state.shape, BF16),
                 jax.ShapeDtypeStruct(pair.shape, BF16),
             ),
-            in_specs=[vmem] * len(args),
-            out_specs=(vmem, vmem),
-            scratch_shapes=[
+            in_specs=[vmem if k in near else far for k in range(len(args))],
+            out_specs=(far, far),
+            scratch_shapes=[pltpu.VMEM(args[k].shape, args[k].dtype) for k in order]
+            + [
+                pltpu.VMEM(pair.shape, BF16),
+                pltpu.VMEM(state.shape, BF16),
+                pltpu.SemaphoreType.DMA((len(order),)),
+                pltpu.SemaphoreType.DMA((2,)),
                 pltpu.VMEM((ns, n, res, ch), BF16),
                 pltpu.VMEM((ch // 128, ns * res, 128), F32),
-                pltpu.VMEM((n, ns, wide + 128), BF16),
-                pltpu.VMEM((n, ns, wide + 128), BF16),
+                pltpu.VMEM((2, ns, span + 128), BF16),
+                pltpu.VMEM((n, ns, span + 128), BF16),
+                pltpu.VMEM((n, 2, ns, span + 128), BF16),
                 pltpu.VMEM((n, ns, wide + 128), BF16),
                 pltpu.VMEM((n, heads, res * res), F32),
                 pltpu.VMEM((n, heads, res * res), F32),
-                pltpu.VMEM((n * ns, wide + 128), F32),
+                pltpu.VMEM((2, n * ns, span + 128), F32),
                 pltpu.VMEM((n * ns, wide + 128), F32),
                 pltpu.VMEM((wide, n * ns), F32),
                 pltpu.VMEM((wide, n * ns), BF16),
@@ -525,7 +690,7 @@
                 pltpu.VMEM((ns, keys), F32),
                 pltpu.VMEM((ns * res, ch), BF16),
             ]
-            + [dma] * 14,
+            + [dma] * 17,
             compiler_params=pltpu.CompilerParams(collective_id=0, has_side_effects=True),
         )(*args)
     )

time: 130 us -> 110 us (0.85)
  the two profiles are of different devices: /device:TPU:87 before, /device:TPU:72 now
where the time goes in v1:
time: 110 us
  Pallas kernels  107 us (97%)
  local copies, waits for them, and re-layouts  2.32 us (2%)
    pallas_call x1, Pallas kernels, per_device(): pl.pallas_call(functools.partial(body, n), out_shape=(jax.ShapeDtypeStruc...  107 us
    unnamed x4, local copies, waits for them, and re-layouts  2.32 us

profile of v1, /device:TPU:72, one launch (start us, length us, event | category | flops | bytes accessed | tf_op | source)
XLA Modules:
  0.0 109.7 jit_solution(13760295782986004395)
XLA Ops:
  0.6 106.7 %shard_map.149 = (bf16[8,32,256]{2,1,0:T(8,128)(2,1)}, bf16[32,32,128]{2,1,0:T(8,128)(2,1)}) custom-call(bf16[8,32,256]{2,1,0:T(8,128)(2,1)} %state_ref.1, bf16[32,32,128]{2,1,0:T(8,128)(2,1)} %pair_hbm.1, s32[8,32]{1,0:T(8,128)} %mask_ref.1, bf16[32,256]{1,0:T(8,128)(2,1)} %bitcast.3, bf16[32,256]{1,0:T(8,128)(2,1)} %bitcast.4, ...), custom_call_target="tpu_custom_call" | custom-call | tf_op jit(solution)/shard_map/pallas_call | solution.py:652
  107.3 0.0 copy-start
  107.3 1.6 %copy.18 = bf16[8,32,256]{2,1,0:T(8,128)(2,1)} copy(bf16[8,32,256]{2,1,0:T(8,128)(2,1)} %get-tuple-element.4) | data formatting | bytes 262144
  108.9 0.0 copy-done
  108.9 0.7 copy.19
Async XLA Ops:
  107.3 1.6 %copy-start = (bf16[32,32,128]{2,1,0:T(8,128)(2,1)S(1)}, bf16[32,32,128]{2,1,0:T(8,128)(2,1)}, u32[]{:S(2)}) copy-start(bf16[32,32,128]{2,1,0:T(8,128)(2,1)} %get-tuple-element.5) | copy-start | bytes 786436

commit v2 on v1

--- a/solution.py
+++ b/solution.py
@@ -69,8 +69,10 @@
     rz,
     tz,
     bx,
-    lf,
-    rf,
+    kt,
+    ka,
+    sel,
+    expand,
     rt,
     rt2,
     lb,
@@ -88,22 +90,22 @@
     vm,
     gated,
     lx_s,
+    lz_s,
+    lf_s,
+    ka_s,
+    rz_s,
+    x_s,
+    tz_s,
+    bx_s,
     lx_r,
-    lz_s,
     lz_r,
-    lf_s,
+    tz_r,
+    rz_r,
+    x1_r,
+    bx_r,
     lf_r,
-    rz_s,
-    rz_r,
-    x1_s,
-    x1_r,
-    xr_s,
-    xf_s,
+    ka_r,
     xf_r,
-    tz_s,
-    tz_r,
-    bx_s,
-    bx_r,
 ):
     a = lax.axis_index("aa")
     b = lax.axis_index("ba")
@@ -120,7 +122,9 @@
     heads = pbw_ref.shape[0]
     wide = res * opm
     per = 128 // opm
-    span = wide // 2
+    parts = 4
+    mine = b % parts
+    span = wide // parts
 
     hbm = (outer_hbm, wq_hbm, wg_hbm, pair_hbm, wk_hbm, wv_hbm, wo_hbm, up_hbm, down_hbm)
     local = (outer_ref, wq_ref, wg_ref, pair_ref, wk_ref, wv_ref, wo_ref, up_ref, down_ref)
@@ -194,10 +198,10 @@
         return (jnp.concatenate(cols, axis=1) * keep_wide).astype(BF16)
 
     left = factor(left_ref)
-    for k in range(2):
+    for k in range(parts):
         ls[k, :, :span] = left[:, k * span : (k + 1) * span]
         ls[k, :, span:] = keep_rep
-    lx[b] = ls[core]
+    lx[b] = ls[mine]
     rz[a, :, :wide] = factor(right_ref)
     rz[a, :, wide:] = keep_rep
 
@@ -207,7 +211,7 @@
         return pltpu.make_async_remote_copy(
             src_ref=src,
             dst_ref=buf,
-            send_sem=ss.at[who],
+            send_sem=ss,
             recv_sem=rs.at[i],
             device_id={"ba": who},
             device_id_type=pl.DeviceIdType.MESH,
@@ -217,31 +221,48 @@
         return pltpu.make_async_remote_copy(
             src_ref=src,
             dst_ref=buf,
-            send_sem=ss.at[who],
+            send_sem=ss,
             recv_sem=rs.at[i],
             device_id={"aa": who},
             device_id_type=pl.DeviceIdType.MESH,
         )
 
     def lx_copy(i, who):
-        return to_row(lx.at[i], ls.at[who % 2], i, who, lx_s, lx_r)
+        return to_row(lx.at[i], ls.at[who % parts], i, who, lx_s, lx_r)
 
     def lz_copy(i, who):
-        return to_col(lz.at[i, core], lx.at[who], i, who, lz_s, lz_r)
-
-    def lf_copy(i, k, src=None):
-        part = lz.at[i, k]
+        return to_col(lz.at[i, mine], lx.at[who, :, pl.ds(0, span)], i, who, lz_s, lz_r)
+
+    def lf_copy(i, q, k, src=None):
+        part = lz.at[i, q]
         return pltpu.make_async_remote_copy(
             src_ref=part if src is None else src,
             dst_ref=part,
-            send_sem=lf_s.at[i],
-            recv_sem=lf_r.at[i],
-            device_id={"ba": partner},
+            send_sem=lf_s,
+            recv_sem=lf_r,
+            device_id={"ba": b - mine + (mine + k) % parts},
+            device_id_type=pl.DeviceIdType.MESH,
+        )
+
+    def ka_copy(who):
+        return pltpu.make_async_remote_copy(
+            src_ref=kt,
+            dst_ref=ka,
+            send_sem=ka_s,
+            recv_sem=ka_r,
+            device_id={"ba": who},
             device_id_type=pl.DeviceIdType.MESH,
         )
 
     def bx_copy(i, who):
-        return to_row(bx.at[i], tz.at[who], i, who, bx_s, bx_r)
+        return pltpu.make_async_remote_copy(
+            src_ref=tz.at[who],
+            dst_ref=bx.at[i],
+            send_sem=bx_s,
+            recv_sem=bx_r.at[i // per],
+            device_id={"ba": who},
+            device_id_type=pl.DeviceIdType.MESH,
+        )
 
     turn = n // 2
 
@@ -251,19 +272,15 @@
         return pltpu.make_async_remote_copy(
             src_ref=part,
             dst_ref=part,
-            send_sem=ss.at[d + step - 1 if way > 0 else turn + d + step - 1],
-            recv_sem=rs.at[i],
+            send_sem=ss,
+            recv_sem=rs(i, d + step, way),
             device_id={"aa": (a + n + way * step) % n},
             device_id_type=pl.DeviceIdType.MESH,
         )
 
-    def spread(buf, ss, rs, d, reach, wait=False):
+    def spread(buf, ss, rs, d, reach):
         def one(step, way):
-            copy = hop(buf, ss, rs, d, step, way)
-            if wait:
-                copy.wait_send()
-            else:
-                copy.start()
+            hop(buf, ss, rs, d, step, way).start()
 
         for step in range(min(reach, turn - d), 0, -1):
             for way in (1, -1):
@@ -283,32 +300,54 @@
                 if d < turn or way > 0:
                     landed((a + n - way * d) % n)
 
-    def ring_sent(buf, ss, rs, reach):
-        for d in range(0, turn, reach):
-            spread(buf, ss, rs, d, reach, wait=True)
+    def tz_at(i, d, way):
+        return tz_r.at[i]
+
+    reach = 4
+    passed = [d for d in range(reach, turn, reach)]
+
+    def rz_at(i, d, way):
+        if d in passed:
+            return rz_r.at[1 + 2 * passed.index(d) + (1 - way) // 2]
+        return rz_r.at[0]
+
+    def all_sent(sem, part):
+        pltpu.make_async_remote_copy(
+            src_ref=part,
+            dst_ref=part,
+            send_sem=sem,
+            recv_sem=sem,
+            device_id={"ba": partner},
+            device_id_type=pl.DeviceIdType.MESH,
+        ).wait_send()
+
+    def all_here(sem, part):
+        pltpu.make_async_remote_copy(
+            src_ref=part,
+            dst_ref=part,
+            send_sem=sem,
+            recv_sem=sem,
+            device_id={"ba": partner},
+            device_id_type=pl.DeviceIdType.MESH,
+        ).wait_recv()
 
     across = chips // 2
 
-    def x_to(i, c, step, way, sem):
+    def x_to(i, c, step, way, d):
         part = rows.at[pl.ds(half * c, half), i]
         who = ((chip + chips + way * step) % chips) * 2 + c
         return pltpu.make_async_remote_copy(
             src_ref=part,
             dst_ref=part,
-            send_sem=sem,
-            recv_sem=x1_r.at[i],
+            send_sem=x_s,
+            recv_sem=x1_r.at[(d + 1) // 2],
             device_id={"ba": who},
             device_id_type=pl.DeviceIdType.MESH,
         )
 
-    def x_first(wait=False):
+    def x_first():
         def one(step, way, c):
-            k = (2 * step - 2 + (1 - way) // 2) * 2 + c
-            copy = x_to(b, c, step, way, x1_s.at[k])
-            if wait:
-                copy.wait_send()
-            else:
-                copy.start()
+            x_to(b, c, step, way, step).start()
 
         for step in range(min(2, across), 0, -1):
             for way in (1, -1):
@@ -318,18 +357,13 @@
                     else:
                         pl.when(core == (1 - way) // 2)(functools.partial(one, step, way, c))
 
-    def x_on(wait=False):
+    def x_on():
         for step in range(min(2, across - 2), 0, -1):
             for way in (1, -1):
                 for c in range(2):
                     if 2 + step < across or c == (1 - way) // 2:
                         i = ((chip + chips - 2 * way) % chips) * 2 + c
-                        k = (2 * step - 2 + (1 - way) // 2) * 2 + c
-                        copy = x_to(i, core, step, way, xr_s.at[k])
-                        if wait:
-                            copy.wait_send()
-                        else:
-                            copy.start()
+                        x_to(i, core, step, way, 2 + step).start()
 
     def x_blocks(first, last):
         return [
@@ -340,28 +374,13 @@
             for c in range(2)
         ]
 
-    def x1_copy(i, who, c):
+    def xf_copy(i, c, sem):
         part = rows.at[pl.ds(half * c, half), i]
-        return to_row(part, part, i, who, x1_s, x1_r)
-
-    def xf_copy(i):
-        part = rows.at[pl.ds(half * core, half), i]
         return pltpu.make_async_remote_copy(
             src_ref=part,
             dst_ref=part,
-            send_sem=xf_s.at[i],
-            recv_sem=xf_r.at[i],
-            device_id={"ba": partner},
-            device_id_type=pl.DeviceIdType.MESH,
-        )
-
-    def in_part(i):
-        part = rows.at[pl.ds(half * (1 - core), half), i]
-        return pltpu.make_async_remote_copy(
-            src_ref=part,
-            dst_ref=part,
-            send_sem=xf_s.at[i],
-            recv_sem=xf_r.at[i],
+            send_sem=x_s,
+            recv_sem=sem,
             device_id={"ba": partner},
             device_id_type=pl.DeviceIdType.MESH,
         )
@@ -372,7 +391,10 @@
 
     lx_copy(b, partner).start()
     lax.fori_loop(0, n - 2, start_l_off, 0)
-    spread(rz, rz_s, rz_r, 0, 4)
+    spread(rz, rz_s, rz_at, 0, reach)
+    x_first()
+    xf_copy(b, 1 - core, xf_r).start()
+    xf_copy(b, core, xf_r).start()
 
     loads[0].wait()
     wf[...] = outer_ref[...].astype(F32)
@@ -388,6 +410,11 @@
 
     lax.fori_loop(0, opm, build, 0)
 
+    lane_e = lax.broadcasted_iota(jnp.int32, (128, res * res), 1)
+    line_e = lax.broadcasted_iota(jnp.int32, (128, res * res), 0)
+    sel[...] = jnp.where(lane_e == line_e * res, 1.0, 0.0).astype(BF16)
+    expand[...] = jnp.where(lane_e // res == line_e, 1.0, 0.0).astype(BF16)
+
     def pass_left(t, _):
         i = row_peer(t)
 
@@ -401,20 +428,20 @@
 
         @pl.when(i == a)
         def _():
-            lz[a, core] = lx[i]
-            lf_copy(a, core, lx.at[i]).start()
-
-        return 0
-
-    def land_right(i):
-        rf[pl.ds(pl.multiple_of(i * ns, ns), ns), :] = rz[i].astype(F32)
+            lz[a, mine] = lx[i, :, :span]
+            for k in range(1, parts):
+                lf_copy(a, mine, k, lx.at[i, :, pl.ds(0, span)]).start()
+
+        return 0
+
+    def nothing(i):
+        pass
 
     lax.fori_loop(0, n * 5 // 8, pass_left, 0)
-    land_right(a)
-    ring(rz, rz_s, rz_r, 4, 1, min(4, turn), land_right)
-    x_first()
-    x1_copy(b, partner, 1 - core).start()
-    xf_copy(b).start()
+    for d in passed:
+        for way in (1, -1):
+            hop(rz, rz_s, rz_at, d, 0, way).wait_recv()
+        spread(rz, rz_s, rz_at, d, reach)
     lax.fori_loop(n * 5 // 8, n, pass_left, 0)
 
     loads[1].wait()
@@ -426,9 +453,28 @@
             [lx[q * per + k, :, span:].astype(F32) for k in range(per)]
         )
 
-    ring(rz, rz_s, rz_r, 4, 5, turn, land_right)
+    def share_left(t, _):
+        i = col_peer(t)
+        lz_copy(i, a).wait_recv()
+        for k in range(1, parts):
+            lf_copy(i, mine, k).start()
+        return 0
+
+    lax.fori_loop(1, n, share_left, 0)
+    all_here(rz_r.at[0], rz.at[pl.ds(0, n - 1 - 2 * len(passed))])
     for q in range(wide // 128):
-        rt[q * 128 : (q + 1) * 128, :] = rf[:, q * 128 : (q + 1) * 128].T
+        block = rz[:, :, q * 128 : (q + 1) * 128].astype(F32).reshape(n * ns, 128)
+        rt[q * 128 : (q + 1) * 128, :] = block.T
+    kt[...] = rz[:, :, wide:].astype(F32).reshape(n * ns, 128).T[:res].astype(BF16)
+
+    def send_keep(t, _):
+        ka_copy((b + t) % n).start()
+        return 0
+
+    @pl.when(a == b)
+    def _():
+        lax.fori_loop(1, n, send_keep, 0)
+        ka[...] = kt[...]
 
     def reorder(d, _):
         rt2[pl.ds(pl.multiple_of(d * res, res), res), :] = rt[
@@ -438,58 +484,45 @@
 
     lax.fori_loop(0, opm, reorder, 0)
 
-    def half_left(i, k):
-        block = lz[i, k].astype(F32)
-        at = pl.ds(pl.multiple_of(i * ns, ns), ns)
-        lf[k, at, :] = block
-
-    def share_left(t, _):
-        i = col_peer(t)
-        lz_copy(i, a).wait_recv()
-        lf_copy(i, core).start()
-        half_left(i, core)
-        return 0
-
-    half_left(a, core)
-    lax.fori_loop(1, n, share_left, 0)
-
-    def land_left(t, _):
-        i = col_peer(t)
-        lf_copy(i, 1 - core).wait_recv()
-        half_left(i, 1 - core)
-        return 0
-
-    lax.fori_loop(0, n, land_left, 0)
+
+    all_here(lf_r, lz.at[:, pl.ds(0, parts - 1)])
+
+    def pass_rows(first, last, then):
+        blocks = x_blocks(first, last)
+        if blocks:
+            many = rows.at[pl.ds(0, half), pl.ds(0, len(blocks))]
+            all_here(x1_r.at[(last + 1) // 2], many)
+        then()
+        for i in blocks:
+            xf_copy(i, core, xf_r).start()
+
+    pass_rows(1, 2, x_on)
 
     groups = res // per
-    for g in range(groups):
-        at = (g % (groups // 2)) * 128
-        lb[g] = lf[g // (groups // 2), :, at : at + 128].astype(BF16)
+    for g in range(groups // 2):
+        at = g * 256 % span
+        block = lz[:, g * 256 // span, :, at : at + 256].astype(F32)
+        lb[g] = block.reshape(n * ns, 256).astype(BF16)
 
     def outer(g, _):
         block = mm(rt2[...], lb[g]).astype(BF16)
-        for d in range(opm):
-            lhs[pl.ds(pl.multiple_of(g * res, res), res), d * 128 : (d + 1) * 128] = block[
-                d * res : (d + 1) * res
-            ]
-        return 0
-
-    lax.fori_loop(0, groups, outer, 0)
+        for k in range(2):
+            at = pl.ds(pl.multiple_of((2 * g + k) * res, res), res)
+            for d in range(opm):
+                lhs[at, d * 128 : (d + 1) * 128] = block[
+                    d * res : (d + 1) * res, k * 128 : (k + 1) * 128
+                ]
+        return 0
+
+    lax.fori_loop(0, groups // 2, outer, 0)
     upd[...] = mm(lhs[...], bd[...])
 
-    def pass_rows(first, last):
-        for i in x_blocks(first, last):
-            x1_copy(i, b, core).wait_recv()
-            if (first, last) == (1, 2):
-                continue
-            xf_copy(i).start()
-
-    pass_rows(1, 2)
-    x_on()
-    for i in x_blocks(1, 2):
-        xf_copy(i).start()
-    count = mm(rf[:, wide:].T.astype(BF16), lf[0, :, span:].astype(BF16))
-    inverse = 1.0 / count[:res]
+
+    @pl.when(a != b)
+    def _():
+        ka_copy(a).wait_recv()
+
+    inverse = 1.0 / mm_nt(kt[...], ka[...])
     loads[3].wait()
     step = 8
     for at in range(0, res, step):
@@ -505,9 +538,23 @@
         fresh = (old + block).astype(BF16)
         pair_out[at : at + step] = fresh.reshape(step, res, cz)
         pn[at * res : (at + step) * res, :] = row_norm(fresh.astype(F32)).astype(BF16)
-    tz[a] = mm_nt(pbw_ref[...], pn[...])
-
-    spread(tz, tz_s, tz_r, 0, 3)
+    tile = mm_nt(pbw_ref[...], pn[...])
+    lane_t = lax.broadcasted_iota(jnp.int32, (heads, 128), 1)
+    base = []
+    for v in range(res // per):
+        top = tile[:, v * 128 : (v + 1) * 128]
+        by = 1
+        while by < res:
+            other = jnp.where(
+                lane_t // by % 2 == 1, pltpu.roll(top, by, 1), pltpu.roll(top, 128 - by, 1)
+            )
+            top = jnp.maximum(top, other)
+            by *= 2
+        base.append(top)
+    base = jnp.concatenate(base, axis=1).astype(BF16)
+    tz[a, :, : res * res] = (tile - base.astype(F32)).astype(BF16)
+    tz[a, :, res * res :] = mm_nt(base, sel[...]).astype(BF16)
+    spread(tz, tz_s, tz_at, 0, 4)
     store = pltpu.make_async_copy(pair_out, pair_hbm_out, store_sem.at[0])
     store.start()
 
@@ -521,16 +568,9 @@
             bx[b] = tz[i]
 
     pass_bias(a)
-    ring(tz, tz_s, tz_r, 3, 1, min(3, turn), pass_bias)
-    pass_rows(3, across)
-    x1_copy(partner, b, core).wait_recv()
-    in_part(partner).wait_recv()
-
-    def land_rows(t, _):
-        in_part(row_peer(t)).wait_recv()
-        return 0
-
-    lax.fori_loop(2, n, land_rows, 0)
+    ring(tz, tz_s, tz_at, 4, 1, min(4, turn), pass_bias)
+    pass_rows(3, 4, lambda: None)
+    all_here(xf_r, rows.at[pl.ds(0, half), pl.ds(0, n)])
     head_lane = lax.broadcasted_iota(jnp.int32, (res, ch), 1) // (ch // heads)
 
     loads[4].wait()
@@ -547,48 +587,41 @@
         sc[s] = mm_nt(query, key)
         return 0
 
-    lax.fori_loop(0, half, score, 0)
-    ring(tz, tz_s, tz_r, 3, 4, min(6, turn), pass_bias)
-    lax.fori_loop(half, ns, score, 0)
-
-    def drain(t, _):
-        lx_copy(b, (b + t) % n).wait_send()
-        lz_copy(a, (a + t) % n).wait_send()
-        return 0
-
-    lax.fori_loop(1, n, drain, 0)
-
-    def drain_left(t, _):
-        lf_copy(t, core).wait_send()
-        return 0
-
-    lax.fori_loop(0, n, drain_left, 0)
-    ring_sent(rz, rz_s, rz_r, 4)
-    x_first(wait=True)
-    x_on(wait=True)
-    x1_copy(b, partner, 1 - core).wait_send()
-
-    def drain_rows(t, _):
-        xf_copy(row_peer(t)).wait_send()
-        return 0
-
-    lax.fori_loop(2, n, drain_rows, 0)
-    xf_copy(b).wait_send()
+    lax.fori_loop(0, ns, score, 0)
+    ring(tz, tz_s, tz_at, 4, 5, turn, pass_bias)
+
+    others = pl.ds(0, n - 1)
+    all_sent(lx_s, lx.at[others])
+    all_sent(lz_s, lz.at[others, 0])
+    all_sent(lf_s, lz.at[:, pl.ds(0, parts - 1)])
+    all_sent(rz_s, rz.at[others])
+    all_sent(x_s, rows.at[:, others])
+
+    @pl.when(a == b)
+    def _():
+        all_sent(ka_s, pn.at[pl.ds(0, (n - 1) * res)])
+
     store.wait()
     for load in loads[6:]:
         load.wait()
-    ring(tz, tz_s, tz_r, 3, 7, turn, pass_bias)
 
     for q in range(n // per):
-        for k in range(per):
-            i = q * per + k
-
-            @pl.when(i != b)
-            def _():
-                bx_copy(i, b).wait_recv()
-
+        @pl.when(b // per == q)
+        def _():
+            all_here(bx_r.at[q], bx.at[pl.ds(0, per - 1)])
+
+        @pl.when(b // per != q)
+        def _():
+            all_here(bx_r.at[q], bx.at[pl.ds(0, per)])
+
+        base = bx[q * per : (q + 1) * per, :, res * res :].astype(F32)
+        base = mm(base.reshape(per * heads, 128).astype(BF16), expand[...])
         for v in range(res // per):
-            cut = [bx[q * per + k, :, v * 128 : (v + 1) * 128] for k in range(per)]
+            cols = slice(v * 128, (v + 1) * 128)
+            cut = [
+                bx[q * per + k, :, cols].astype(F32) + base[k * heads : (k + 1) * heads, cols]
+                for k in range(per)
+            ]
             turned = [cut[0]] + [pltpu.roll(cut[k], opm * k, 1) for k in range(1, per)]
             for m in range(per):
                 mixed = pick([turned[(k - m) % per] for k in range(per)])
@@ -615,7 +648,7 @@
         gated[at, :] = (out * gs[at, :]).astype(BF16)
         return 0
 
-    lax.fori_loop(0, ns, attend, 0)
+    lax.fori_loop(0, ns, attend, 0, unroll=2)
 
     middle = state_ref[...].reshape(ns * res, ch).astype(F32) + mm(gated[...], wo_ref[...])
     hidden = jnp.maximum(mm(row_norm(middle).astype(BF16), up_ref[...]), 0.0).astype(BF16)
@@ -623,13 +656,8 @@
     msa_out[...] = final.astype(BF16).reshape(ns, res, ch)
     store = pltpu.make_async_copy(msa_out, msa_hbm_out, store_sem.at[1])
     store.start()
-    ring_sent(tz, tz_s, tz_r, 3)
-
-    def drain_bias(t, _):
-        bx_copy(b, (b + t) % n).wait_send()
-        return 0
-
-    lax.fori_loop(1, n, drain_bias, 0)
+    all_sent(tz_s, tz.at[others])
+    all_sent(bx_s, bx.at[others])
     store.wait()
 
 
@@ -639,7 +667,8 @@
     opm, heads, cz = left.shape[1], pbw.shape[1], pair.shape[2]
     args = args[:3] + (left.T, args[4].T, args[5], pbw.T) + args[7:]
     wide = res * opm
-    span = wide // 2
+    parts = 4
+    span = wide // parts
     per = 128 // opm
     groups = res // per
     keys = n * res
@@ -665,17 +694,19 @@
                 pltpu.SemaphoreType.DMA((2,)),
                 pltpu.VMEM((ns, n, res, ch), BF16),
                 pltpu.VMEM((ch // 128, ns * res, 128), F32),
-                pltpu.VMEM((2, ns, span + 128), BF16),
+                pltpu.VMEM((parts, ns, span + 128), BF16),
                 pltpu.VMEM((n, ns, span + 128), BF16),
-                pltpu.VMEM((n, 2, ns, span + 128), BF16),
+                pltpu.VMEM((n, parts, ns, span), BF16),
                 pltpu.VMEM((n, ns, wide + 128), BF16),
-                pltpu.VMEM((n, heads, res * res), F32),
-                pltpu.VMEM((n, heads, res * res), F32),
-                pltpu.VMEM((2, n * ns, span + 128), F32),
-                pltpu.VMEM((n * ns, wide + 128), F32),
+                pltpu.VMEM((n, heads, res * res + 128), BF16),
+                pltpu.VMEM((n, heads, res * res + 128), BF16),
+                pltpu.VMEM((res, n * ns), BF16),
+                pltpu.VMEM((res, n * ns), BF16),
+                pltpu.VMEM((128, res * res), BF16),
+                pltpu.VMEM((128, res * res), BF16),
                 pltpu.VMEM((wide, n * ns), F32),
                 pltpu.VMEM((wide, n * ns), BF16),
-                pltpu.VMEM((groups, n * ns, 128), BF16),
+                pltpu.VMEM((groups // 2, n * ns, 256), BF16),
                 pltpu.VMEM((opm * opm, cz), F32),
                 pltpu.VMEM((opm * 128, per * cz), BF16),
                 pltpu.VMEM((groups * res, opm * 128), BF16),
@@ -690,7 +721,11 @@
                 pltpu.VMEM((ns, keys), F32),
                 pltpu.VMEM((ns * res, ch), BF16),
             ]
-            + [dma] * 17,
+            + [pltpu.SemaphoreType.DMA] * 8
+            + [dma] * 3
+            + [pltpu.SemaphoreType.DMA((3,))] * 2
+            + [pltpu.SemaphoreType.DMA((n // per,))]
+            + [pltpu.SemaphoreType.DMA] * 3,
             compiler_params=pltpu.CompilerParams(collective_id=0, has_side_effects=True),
         )(*args)
     )

time: 110 us -> 98.4 us (0.89)
  the two profiles are of different devices: /device:TPU:72 before, /device:TPU:87 now
where the time goes in v2:
time: 98.4 us; the launch traced here: 98.2 us
  Pallas kernels  95.2 us (97%)
  local copies, waits for them, and re-layouts  2.32 us (2%)
    pallas_call x1, Pallas kernels, per_device(): pl.pallas_call(functools.partial(body, n), out_shape=(jax.ShapeDtypeStruc...  95.2 us
    unnamed x4, local copies, waits for them, and re-layouts  2.32 us

profile of v2, /device:TPU:87, one launch (start us, length us, event | category | flops | bytes accessed | tf_op | source)
XLA Modules:
  0.0 98.2 jit_solution(12083446208061847302)
XLA Ops:
  0.6 95.2 %shard_map.149 = (bf16[8,32,256]{2,1,0:T(8,128)(2,1)}, bf16[32,32,128]{2,1,0:T(8,128)(2,1)}) custom-call(bf16[8,32,256]{2,1,0:T(8,128)(2,1)} %state_ref.1, bf16[32,32,128]{2,1,0:T(8,128)(2,1)} %pair_hbm.1, s32[8,32]{1,0:T(8,128)} %mask_ref.1, bf16[32,256]{1,0:T(8,128)(2,1)} %bitcast.3, bf16[32,256]{1,0:T(8,128)(2,1)} %bitcast.4, ...), custom_call_target="tpu_custom_call" | custom-call | tf_op jit(solution)/shard_map/pallas_call | solution.py:681
  95.9 0.0 copy-start
  95.9 1.6 %copy.18 = bf16[8,32,256]{2,1,0:T(8,128)(2,1)} copy(bf16[8,32,256]{2,1,0:T(8,128)(2,1)} %get-tuple-element.4) | data formatting | bytes 262144
  97.5 0.0 copy-done
  97.5 0.7 copy.19
Async XLA Ops:
  95.9 1.6 %copy-start = (bf16[32,32,128]{2,1,0:T(8,128)(2,1)S(1)}, bf16[32,32,128]{2,1,0:T(8,128)(2,1)}, u32[]{:S(2)}) copy-start(bf16[32,32,128]{2,1,0:T(8,128)(2,1)} %get-tuple-element.5) | copy-start | bytes 786436

commit v3 on v2

--- a/solution.py
+++ b/solution.py
@@ -32,13 +32,13 @@
 
 def body(
     n,
-    state_ref,
+    state_hbm,
     pair_hbm,
-    mask_ref,
-    left_ref,
-    right_ref,
+    mask_hbm,
+    left_hbm,
+    right_hbm,
     outer_hbm,
-    pbw_ref,
+    pbw_hbm,
     wq_hbm,
     wk_hbm,
     wv_hbm,
@@ -48,6 +48,11 @@
     down_hbm,
     msa_hbm_out,
     pair_hbm_out,
+    state_ref,
+    mask_ref,
+    left_ref,
+    right_ref,
+    pbw_ref,
     pair_ref,
     outer_ref,
     wq_ref,
@@ -126,8 +131,14 @@
     mine = b % parts
     span = wide // parts
 
+    first = (state_hbm, mask_hbm, left_hbm, right_hbm, pbw_hbm)
     hbm = (outer_hbm, wq_hbm, wg_hbm, pair_hbm, wk_hbm, wv_hbm, wo_hbm, up_hbm, down_hbm)
+    first_to = (state_ref, mask_ref, left_ref, right_ref, pbw_ref)
     local = (outer_ref, wq_ref, wg_ref, pair_ref, wk_ref, wv_ref, wo_ref, up_ref, down_ref)
+    firsts = [
+        pltpu.make_async_copy(src, dst, load_sem.at[len(hbm) + k])
+        for k, (src, dst) in enumerate(zip(first, first_to))
+    ]
     loads = [
         pltpu.make_async_copy(src, dst, load_sem.at[k])
         for k, (src, dst) in enumerate(zip(hbm, local))
@@ -140,6 +151,8 @@
     def col_peer(t):
         return (a + near_to_far(t) + n) % n
 
+    for load in firsts:
+        load.start()
     barrier = pltpu.get_barrier_semaphore()
 
     def greet(t, _):
@@ -156,6 +169,8 @@
     for load in loads:
         load.start()
 
+    for load in firsts:
+        load.wait()
     state = state_ref[...].reshape(ns * res, ch).astype(F32)
     normed = row_norm(state).astype(BF16)
     rows[:, b] = normed.reshape(ns, res, ch)
@@ -259,7 +274,7 @@
             src_ref=tz.at[who],
             dst_ref=bx.at[i],
             send_sem=bx_s,
-            recv_sem=bx_r.at[i // per],
+            recv_sem=bx_r,
             device_id={"ba": who},
             device_id_type=pl.DeviceIdType.MESH,
         )
@@ -485,8 +500,6 @@
     lax.fori_loop(0, opm, reorder, 0)
 
 
-    all_here(lf_r, lz.at[:, pl.ds(0, parts - 1)])
-
     def pass_rows(first, last, then):
         blocks = x_blocks(first, last)
         if blocks:
@@ -497,6 +510,7 @@
             xf_copy(i, core, xf_r).start()
 
     pass_rows(1, 2, x_on)
+    all_here(lf_r, lz.at[:, pl.ds(0, parts - 1)])
 
     groups = res // per
     for g in range(groups // 2):
@@ -558,6 +572,7 @@
     store = pltpu.make_async_copy(pair_out, pair_hbm_out, store_sem.at[0])
     store.start()
 
+    pass_rows(3, 4, lambda: None)
     def pass_bias(i):
         @pl.when(i != b)
         def _():
@@ -569,7 +584,6 @@
 
     pass_bias(a)
     ring(tz, tz_s, tz_at, 4, 1, min(4, turn), pass_bias)
-    pass_rows(3, 4, lambda: None)
     all_here(xf_r, rows.at[pl.ds(0, half), pl.ds(0, n)])
     head_lane = lax.broadcasted_iota(jnp.int32, (res, ch), 1) // (ch // heads)
 
@@ -587,7 +601,7 @@
         sc[s] = mm_nt(query, key)
         return 0
 
-    lax.fori_loop(0, ns, score, 0)
+    lax.fori_loop(0, ns, score, 0, unroll=2)
     ring(tz, tz_s, tz_at, 4, 5, turn, pass_bias)
 
     others = pl.ds(0, n - 1)
@@ -605,21 +619,15 @@
     for load in loads[6:]:
         load.wait()
 
+    all_here(bx_r, bx.at[others])
+    base = bx[:, :, res * res :].astype(F32).reshape(n * heads, 128).astype(BF16)
+    base = mm(base, expand[...])
     for q in range(n // per):
-        @pl.when(b // per == q)
-        def _():
-            all_here(bx_r.at[q], bx.at[pl.ds(0, per - 1)])
-
-        @pl.when(b // per != q)
-        def _():
-            all_here(bx_r.at[q], bx.at[pl.ds(0, per)])
-
-        base = bx[q * per : (q + 1) * per, :, res * res :].astype(F32)
-        base = mm(base.reshape(per * heads, 128).astype(BF16), expand[...])
         for v in range(res // per):
             cols = slice(v * 128, (v + 1) * 128)
             cut = [
-                bx[q * per + k, :, cols].astype(F32) + base[k * heads : (k + 1) * heads, cols]
+                bx[q * per + k, :, cols].astype(F32)
+                + base[(q * per + k) * heads : (q * per + k + 1) * heads, cols]
                 for k in range(per)
             ]
             turned = [cut[0]] + [pltpu.roll(cut[k], opm * k, 1) for k in range(1, per)]
@@ -648,7 +656,7 @@
         gated[at, :] = (out * gs[at, :]).astype(BF16)
         return 0
 
-    lax.fori_loop(0, ns, attend, 0, unroll=2)
+    lax.fori_loop(0, ns, attend, 0, unroll=4)
 
     middle = state_ref[...].reshape(ns * res, ch).astype(F32) + mm(gated[...], wo_ref[...])
     hidden = jnp.maximum(mm(row_norm(middle).astype(BF16), up_ref[...]), 0.0).astype(BF16)
@@ -675,8 +683,7 @@
     dma = pltpu.SemaphoreType.DMA((n,))
     vmem = pl.BlockSpec(memory_space=pltpu.VMEM)
     far = pl.BlockSpec(memory_space=pl.ANY)
-    near = (0, 2, 3, 4, 6)
-    order = (1, 5, 7, 8, 9, 10, 11, 12, 13)
+    order = (0, 2, 3, 4, 6, 1, 5, 7, 8, 9, 10, 11, 12, 13)
     return tuple(
         pl.pallas_call(
             functools.partial(body, n),
@@ -684,7 +691,7 @@
                 jax.ShapeDtypeStruct(state.shape, BF16),
                 jax.ShapeDtypeStruct(pair.shape, BF16),
             ),
-            in_specs=[vmem if k in near else far for k in range(len(args))],
+            in_specs=[far] * len(args),
             out_specs=(far, far),
             scratch_shapes=[pltpu.VMEM(args[k].shape, args[k].dtype) for k in order]
             + [
@@ -724,10 +731,11 @@
             + [pltpu.SemaphoreType.DMA] * 8
             + [dma] * 3
             + [pltpu.SemaphoreType.DMA((3,))] * 2
-            + [pltpu.SemaphoreType.DMA((n // per,))]
-            + [pltpu.SemaphoreType.DMA] * 3,
-            compiler_params=pltpu.CompilerParams(collective_id=0, has_side_effects=True),
-        )(*args)
+            + [pltpu.SemaphoreType.DMA] * 4,
+            compiler_params=pltpu.CompilerParams(
+                collective_id=0, has_side_effects=True, vmem_limit_bytes=52 * 1024 * 1024
+            ),
+        )(*[pltpu.with_memory_space_constraint(x, pltpu.HBM) for x in args])
     )
 
 

time: 98.4 us -> 95.3 us (0.968)
  Pallas kernels: 95.2 us -> 93.2 us
    pallas_call x1, Pallas kernels: 95.2 us -> 93.2 us  [per_device(): pl.pallas_call(functools.partial(body, n), out_shape=(jax.ShapeDtypeStruc...]
    unnamed x4 -> x2, local copies, waits for them, and re-layouts: 2.32 us -> 1.36 us
where the time goes in v3:
time: 95.3 us; the launch traced here: 95.2 us
  Pallas kernels  93.2 us (98%)
  local copies, waits for them, and re-layouts  1.36 us (1%)
    pallas_call x1, Pallas kernels, per_device(): pl.pallas_call(functools.partial(body, n), out_shape=(jax.ShapeDtypeStruc...  93.2 us

profile of v3, /device:TPU:87, one launch (start us, length us, event | category | flops | bytes accessed | tf_op | source)
XLA Modules:
  0.0 95.2 jit_solution(17419604611416388580)
XLA Ops:
  0.6 93.2 %shard_map.149 = (bf16[8,32,256]{2,1,0:T(8,128)(2,1)S(1)}, bf16[32,32,128]{2,1,0:T(8,128)(2,1)S(1)}) custom-call(bf16[8,32,256]{2,1,0:T(8,128)(2,1)} %state_hbm.1, bf16[32,32,128]{2,1,0:T(8,128)(2,1)} %pair_hbm.1, s32[8,32]{1,0:T(8,128)} %mask_hbm.1, bf16[32,256]{1,0:T(8,128)(2,1)} %bitcast.3, bf16[32,256]{1,0:T(8,128)(2,1)} %bitcast.4, ...), custom_call_target="tpu_custom_call" | custom-call | tf_op jit(solution)/shard_map/pallas_call | solution.py:688
  93.8 0.7 copy.18
  94.5 0.7 copy.19

commit v4 on v3

--- a/solution.py
+++ b/solution.py
@@ -80,7 +80,6 @@
     expand,
     rt,
     rt2,
-    lb,
     wf,
     bd,
     lhs,
@@ -93,7 +92,6 @@
     qs,
     gs,
     vm,
-    gated,
     lx_s,
     lz_s,
     lf_s,
@@ -453,11 +451,12 @@
         pass
 
     lax.fori_loop(0, n * 5 // 8, pass_left, 0)
+    lax.fori_loop(n * 5 // 8, n, pass_left, 0)
+
     for d in passed:
         for way in (1, -1):
             hop(rz, rz_s, rz_at, d, 0, way).wait_recv()
         spread(rz, rz_s, rz_at, d, reach)
-    lax.fori_loop(n * 5 // 8, n, pass_left, 0)
 
     loads[1].wait()
     loads[2].wait()
@@ -477,9 +476,6 @@
 
     lax.fori_loop(1, n, share_left, 0)
     all_here(rz_r.at[0], rz.at[pl.ds(0, n - 1 - 2 * len(passed))])
-    for q in range(wide // 128):
-        block = rz[:, :, q * 128 : (q + 1) * 128].astype(F32).reshape(n * ns, 128)
-        rt[q * 128 : (q + 1) * 128, :] = block.T
     kt[...] = rz[:, :, wide:].astype(F32).reshape(n * ns, 128).T[:res].astype(BF16)
 
     def send_keep(t, _):
@@ -490,6 +486,10 @@
     def _():
         lax.fori_loop(1, n, send_keep, 0)
         ka[...] = kt[...]
+
+    for q in range(wide // 128):
+        block = rz[:, :, q * 128 : (q + 1) * 128].astype(F32).reshape(n * ns, 128)
+        rt[q * 128 : (q + 1) * 128, :] = block.T
 
     def reorder(d, _):
         rt2[pl.ds(pl.multiple_of(d * res, res), res), :] = rt[
@@ -510,25 +510,21 @@
             xf_copy(i, core, xf_r).start()
 
     pass_rows(1, 2, x_on)
-    all_here(lf_r, lz.at[:, pl.ds(0, parts - 1)])
-
-    groups = res // per
-    for g in range(groups // 2):
-        at = g * 256 % span
-        block = lz[:, g * 256 // span, :, at : at + 256].astype(F32)
-        lb[g] = block.reshape(n * ns, 256).astype(BF16)
-
-    def outer(g, _):
-        block = mm(rt2[...], lb[g]).astype(BF16)
-        for k in range(2):
-            at = pl.ds(pl.multiple_of((2 * g + k) * res, res), res)
+    def outer(k, _):
+        g = (mine + k) % parts
+        left = lz[:, g].astype(F32).reshape(n * ns, span).astype(BF16)
+        block = mm(rt2[...], left).astype(BF16)
+        for k in range(span // 128):
+            at = pl.ds(pl.multiple_of((span // 128 * g + k) * res, res), res)
             for d in range(opm):
                 lhs[at, d * 128 : (d + 1) * 128] = block[
                     d * res : (d + 1) * res, k * 128 : (k + 1) * 128
                 ]
         return 0
 
-    lax.fori_loop(0, groups // 2, outer, 0)
+    outer(0, 0)
+    all_here(lf_r, lz.at[:, pl.ds(0, parts - 1)])
+    lax.fori_loop(1, parts, outer, 0)
     upd[...] = mm(lhs[...], bd[...])
 
 
@@ -642,9 +638,8 @@
                 q, pl.ds(h, res, stride=heads), :
             ]
 
-    def attend(s, _):
-        valid = vm[pl.ds(s, 1), :]
-        scores = jnp.where(valid > 0, sc[s] + bh[...], -1000000000.0)
+    def attend(s):
+        scores = jnp.where(vm[s : s + 1, :] > 0, sc[s] + bh[...], -1000000000.0)
         top = jnp.max(scores, axis=-1, keepdims=True)
         raw = jnp.exp(scores - top)
         mass = jnp.sum(raw, axis=-1, keepdims=True)
@@ -652,21 +647,25 @@
         out = mixed[:res]
         for h in range(1, heads):
             out = jnp.where(head_lane == h, mixed[h * res : (h + 1) * res], out)
-        at = pl.ds(pl.multiple_of(s * res, res), res)
-        gated[at, :] = (out * gs[at, :]).astype(BF16)
-        return 0
-
-    lax.fori_loop(0, ns, attend, 0, unroll=4)
-
-    middle = state_ref[...].reshape(ns * res, ch).astype(F32) + mm(gated[...], wo_ref[...])
-    hidden = jnp.maximum(mm(row_norm(middle).astype(BF16), up_ref[...]), 0.0).astype(BF16)
-    final = middle + mm(hidden, down_ref[...])
-    msa_out[...] = final.astype(BF16).reshape(ns, res, ch)
-    store = pltpu.make_async_copy(msa_out, msa_hbm_out, store_sem.at[1])
-    store.start()
+        return (out * gs[s * res : (s + 1) * res, :]).astype(BF16)
+
+    stores = []
+    for k in range(2):
+        these = slice(k * half, (k + 1) * half)
+        gated = jnp.concatenate([attend(s) for s in range(k * half, (k + 1) * half)], axis=0)
+        middle = state_ref[these].reshape(half * res, ch).astype(F32) + mm(gated, wo_ref[...])
+        hidden = jnp.maximum(mm(row_norm(middle).astype(BF16), up_ref[...]), 0.0).astype(BF16)
+        final = middle + mm(hidden, down_ref[...])
+        msa_out[these] = final.astype(BF16).reshape(half, res, ch)
+        at = pl.ds(k * half, half)
+        stores.append(
+            pltpu.make_async_copy(msa_out.at[at], msa_hbm_out.at[at], store_sem.at[1 + k])
+        )
+        stores[k].start()
     all_sent(tz_s, tz.at[others])
     all_sent(bx_s, bx.at[others])
-    store.wait()
+    for store in stores:
+        store.wait()
 
 
 def per_device(n, *args):
@@ -698,7 +697,7 @@
                 pltpu.VMEM(pair.shape, BF16),
                 pltpu.VMEM(state.shape, BF16),
                 pltpu.SemaphoreType.DMA((len(order),)),
-                pltpu.SemaphoreType.DMA((2,)),
+                pltpu.SemaphoreType.DMA((3,)),
                 pltpu.VMEM((ns, n, res, ch), BF16),
                 pltpu.VMEM((ch // 128, ns * res, 128), F32),
                 pltpu.VMEM((parts, ns, span + 128), BF16),
@@ -713,7 +712,6 @@
                 pltpu.VMEM((128, res * res), BF16),
                 pltpu.VMEM((wide, n * ns), F32),
                 pltpu.VMEM((wide, n * ns), BF16),
-                pltpu.VMEM((groups // 2, n * ns, 256), BF16),
                 pltpu.VMEM((opm * opm, cz), F32),
                 pltpu.VMEM((opm * 128, per * cz), BF16),
                 pltpu.VMEM((groups * res, opm * 128), BF16),
@@ -726,7 +724,6 @@
                 pltpu.VMEM((ns * res, ch), BF16),
                 pltpu.VMEM((ns * res, ch), F32),
                 pltpu.VMEM((ns, keys), F32),
-                pltpu.VMEM((ns * res, ch), BF16),
             ]
             + [pltpu.SemaphoreType.DMA] * 8
             + [dma] * 3

time: 95.3 us -> 94 us (0.986)
  the two profiles are of different devices: /device:TPU:87 before, /device:TPU:71 now
where the time goes in v4:
time: 94 us; the launch traced here: 93.9 us
  Pallas kernels  91.9 us (98%)
  local copies, waits for them, and re-layouts  1.36 us (1%)
    pallas_call x1, Pallas kernels, per_device(): pl.pallas_call(functools.partial(body, n), out_shape=(jax.ShapeDtypeStruc...  91.9 us

profile of v4, /device:TPU:71, one launch (start us, length us, event | category | flops | bytes accessed | tf_op | source)
XLA Modules:
  0.0 93.9 jit_solution(9977280249635124525)
XLA Ops:
  0.6 91.9 %shard_map.149 = (bf16[8,32,256]{2,1,0:T(8,128)(2,1)S(1)}, bf16[32,32,128]{2,1,0:T(8,128)(2,1)S(1)}) custom-call(bf16[8,32,256]{2,1,0:T(8,128)(2,1)} %state_hbm.1, bf16[32,32,128]{2,1,0:T(8,128)(2,1)} %pair_hbm.1, s32[8,32]{1,0:T(8,128)} %mask_hbm.1, bf16[32,256]{1,0:T(8,128)(2,1)} %bitcast.3, bf16[32,256]{1,0:T(8,128)(2,1)} %bitcast.4, ...), custom_call_target="tpu_custom_call" | custom-call | tf_op jit(solution)/shard_map/pallas_call | solution.py:687
  92.5 0.7 copy.18
  93.2 0.7 copy.19

commit v5 on v4

--- a/solution.py
+++ b/solution.py
@@ -564,7 +564,7 @@
     base = jnp.concatenate(base, axis=1).astype(BF16)
     tz[a, :, : res * res] = (tile - base.astype(F32)).astype(BF16)
     tz[a, :, res * res :] = mm_nt(base, sel[...]).astype(BF16)
-    spread(tz, tz_s, tz_at, 0, 4)
+    spread(tz, tz_s, tz_at, 0, 3)
     store = pltpu.make_async_copy(pair_out, pair_hbm_out, store_sem.at[0])
     store.start()
 
@@ -579,7 +579,7 @@
             bx[b] = tz[i]
 
     pass_bias(a)
-    ring(tz, tz_s, tz_at, 4, 1, min(4, turn), pass_bias)
+    ring(tz, tz_s, tz_at, 3, 1, min(3, turn), pass_bias)
     all_here(xf_r, rows.at[pl.ds(0, half), pl.ds(0, n)])
     head_lane = lax.broadcasted_iota(jnp.int32, (res, ch), 1) // (ch // heads)
 
@@ -598,7 +598,7 @@
         return 0
 
     lax.fori_loop(0, ns, score, 0, unroll=2)
-    ring(tz, tz_s, tz_at, 4, 5, turn, pass_bias)
+    ring(tz, tz_s, tz_at, 3, 4, turn, pass_bias)
 
     others = pl.ds(0, n - 1)
     all_sent(lx_s, lx.at[others])

time: 94 us -> 93.2 us (level)
  no operation moved by 1% of the time
where the time goes in v5:
time: 93.2 us; the launch traced here: 93 us
  Pallas kernels  91 us (98%)
  local copies, waits for them, and re-layouts  1.36 us (1%)
    pallas_call x1, Pallas kernels, per_device(): pl.pallas_call(functools.partial(body, n), out_shape=(jax.ShapeDtypeStruc...  91 us

profile of v5, /device:TPU:71, one launch (start us, length us, event | category | flops | bytes accessed | tf_op | source)
XLA Modules:
  0.0 93.0 jit_solution(13748627072955702963)
XLA Ops:
  0.6 91.0 %shard_map.149 = (bf16[8,32,256]{2,1,0:T(8,128)(2,1)S(1)}, bf16[32,32,128]{2,1,0:T(8,128)(2,1)S(1)}) custom-call(bf16[8,32,256]{2,1,0:T(8,128)(2,1)} %state_hbm.1, bf16[32,32,128]{2,1,0:T(8,128)(2,1)} %pair_hbm.1, s32[8,32]{1,0:T(8,128)} %mask_hbm.1, bf16[32,256]{1,0:T(8,128)(2,1)} %bitcast.3, bf16[32,256]{1,0:T(8,128)(2,1)} %bitcast.4, ...), custom_call_target="tpu_custom_call" | custom-call | tf_op jit(solution)/shard_map/pallas_call | solution.py:687
  91.7 0.7 copy.18
  92.3 0.7 copy.19
